TPU v7x, 256 devices: a whole 4x4x8 slice. The times are simulated.
256 devices in a mesh: branch: 2 (over z_lo), batch: 32 (over y, z_hi, core), rows: 4 (over x).
Axes of the slice: x: 4, y: 4, z: 8 (z_hi: 4, z_lo: 2; z = z_hi * 2 + z_lo), core: 2. Of those that a mesh axis runs over, the one named last changes fastest.
Arguments:
- timestep: int32 [32], P('batch'), parts along dimension 0, may hold values from 0 to 999
- features: bfloat16 [32, 2, 32, 64, 640], P('batch', 'branch', 'rows'), parts along dimension 0, may hold values from -6 to 6
- conv1_weight: bfloat16 [2, 3, 3, 640, 640], P('branch', None, None, None, 'rows'), may hold values from -0.078125 to 0.078125
- conv1_bias: float32 [2, 640], P('branch'), may hold values from -3 to 3
- conv2_weight: bfloat16 [2, 3, 3, 640, 640], P('branch', None, None, None, 'rows'), may hold values from -0.078125 to 0.078125
- conv2_bias: float32 [2, 640], P('branch'), may hold values from -3 to 3
- norm1_gain: float32 [2, 640], P('branch'), may hold values from 0.25 to 1.75
- norm1_shift: float32 [2, 640], P('branch'), may hold values from -3 to 3
- norm2_gain: float32 [2, 640], P('branch'), may hold values from 0.25 to 1.75
- norm2_shift: float32 [2, 640], P('branch'), may hold values from -3 to 3
- time_weight: bfloat16 [2, 320, 1280], P('branch'), may hold values from -0.3125 to 0.3125
- emb_weight: bfloat16 [2, 1280, 640], P('branch'), may hold values from -0.15625 to 0.15625
- zero_weight: bfloat16 [640, 640], replicated, may hold values from -0.25 to 0.25
- zero_bias: float32 [640], replicated, may hold values from -3 to 3
Outputs:
- block_out: bfloat16 [32, 2, 32, 64, 640], P('batch', 'branch', 'rows'), parts along dimension 0
There are 32 independent parts, one for each index of `batch`. A program takes and returns all parts, laid end to end along the dimension named above; an argument that names none is the same for every part. Nothing has to cross between parts.
All inputs are finite; a program needn't handle non-finite values.
Results may differ from a plain program's by a relative error of at most 0.01.
Values may be sent and summed in bfloat16 or wider, within the bound.
A program may use at most 128 MiB of HBM per device.

v0:
```python
import functools
import math

import numpy as np

import jax
import jax.numpy as jnp
from jax import lax
from jax.experimental import pallas as pl
from jax.experimental.pallas import tpu as pltpu
from jax.sharding import PartitionSpec as P

C = 640
GROUP = 20
W = 64
HR = 8
POS = HR * W
QC = 160
COUNT = 2048 * GROUP
CTL = 140
MESH = pl.DeviceIdType.MESH
F32 = jnp.float32
BF16 = jnp.bfloat16


ORDER = (
    ("own", 0, "N1", "P", 0),
    ("own", 0, "N2", "P", 0),
    ("own", 0, "N1", "P", 1),
    ("own", 0, "N2", "P", 1),
    ("own", 0, "N1", "P", 2),
    ("own", 0, "N2", "P", 2),
    ("stats",),
    ("time",),
    ("piece", 0, "N1", 0),
    ("piece", 0, "N2", 0),
    ("piece", 0, "N1", 1),
    ("piece", 0, "N2", 1),
    ("edges",),
    ("piece", 0, "N1", 2),
    ("piece", 0, "N2", 2),
    ("own", 0, "N1", "C", 0),
    ("own", 0, "N2", "C", 0),
    ("own", 0, "N1", "C", 1),
    ("own", 0, "N2", "C", 1),
    ("own", 0, "N1", "C", 2),
    ("own", 0, "N2", "C", 2),
    ("own", 1, "N1", "P", 0),
    ("own", 1, "N2", "P", 0),
    ("piece", 0, "F", 0),
    ("piece", 0, "F", 1),
    ("piece", 0, "F", 2),
    ("first",),
    ("c", 0, "N1", 0),
    ("c", 0, "N2", 0),
    ("zlate0",),
    ("block", 0, "N1", 0),
    ("block", 0, "N2", 0),
    ("c", 0, "N1", 1),
    ("block", 0, "N1", 1),
    ("c", 0, "N2", 1),
    ("block", 0, "N2", 1),
    ("conv", 0, "N1", 0),
    ("c", 0, "N1", 2),
    ("c", 0, "N2", 2),
    ("block", 0, "N1", 2),
    ("block", 0, "N2", 2),
    ("own", 1, "N1", "P", 2),
    ("own", 1, "N2", "P", 1),
    ("conv", 0, "N1", 1),
    ("piece", 1, "N1", 0),
    ("conv", 0, "N2", 0),
    ("piece", 1, "N2", 0),
    ("conv", 0, "N1", 2),
    ("block", 0, "F", 0),
    ("block", 0, "F", 1),
    ("hidden", "N1"),
    ("conv", 0, "N2", 1),
    ("block", 0, "F", 2),
    ("own", 1, "N1", "P", 1),
    ("own", 1, "N2", "P", 2),
    ("own", 1, "N1", "C", 0),
    ("own", 1, "N2", "C", 1),
    ("piece", 1, "N2", 1),
    ("conv", 0, "N2", 2),
    ("hidden", "N2"),
    ("piece", 1, "N1", 2),
    ("conv", 0, "F", 0),
    ("piece", 1, "F", 0),
    ("conv", 0, "F", 1),
    ("conv", 0, "F", 2),
    ("hidden", "F"),
    ("piece", 1, "N1", 1),
    ("own", 1, "N1", "C", 1),
    ("own", 1, "N2", "C", 0),
    ("own", 1, "N1", "C", 2),
    ("own", 1, "N2", "C", 2),
    ("piece", 1, "N2", 2),
    ("c", 1, "N1", 0),
    ("block", 1, "N1", 0),
    ("c", 1, "N2", 1),
    ("block", 1, "N2", 1),
    ("second",),
    ("c", 1, "N1", 1),
    ("piece", 1, "F", 1),
    ("block", 1, "N1", 1),
    ("conv", 1, "N1", 0),
    ("c", 1, "N1", 2),
    ("block", 1, "N1", 2),
    ("c", 1, "N2", 0),
    ("block", 1, "N2", 0),
    ("conv", 1, "N1", 1),
    ("c", 1, "N2", 2),
    ("piece", 1, "F", 2),
    ("block", 1, "N2", 2),
    ("conv", 1, "N1", 2),
    ("conv", 1, "N2", 0),
    ("block", 1, "F", 0),
    ("conv", 1, "N2", 1),
    ("conv", 1, "N2", 2),
    ("block", 1, "F", 1),
    ("conv", 1, "F", 0),
    ("conv", 1, "F", 1),
    ("block", 1, "F", 2),
    ("conv", 1, "F", 2),
)
AHEAD = {
    (0, "N1", 2),
    (0, "N2", 2),
    (0, "F", 1),
    (0, "F", 2),
    (1, "N1", 0),
    (1, "N1", 1),
    (1, "N1", 2),
    (1, "N2", 0),
    (1, "N2", 1),
    (1, "N2", 2),
}


def group_of(c):
    return (c * 3277) >> 16


def iota(shape, dim):
    return lax.broadcasted_iota(jnp.int32, shape, dim)


def split3(x):
    hi = x.astype(BF16).astype(F32)
    left = x - hi
    mid = left.astype(BF16).astype(F32)
    return jnp.concatenate([hi, mid, left - mid], axis=0).astype(BF16)


def exact_dot(x, m):
    out = jnp.dot(split3(x), m, preferred_element_type=F32)
    return out[0:8] + out[8:16] + out[16:24]


def silu(x):
    h = 0.5 * x
    return h + h * jnp.tanh(h)


class Links:
    def __init__(self, send, recv):
        self.send, self.recv = send, recv
        self.keys, self.started, self.count = {}, [], 0

    def slot(self, key):
        return self.keys.setdefault(key, len(self.keys))

    def prepare(self, key, src, dst, device):
        copy = pltpu.make_async_remote_copy(
            src_ref=src,
            dst_ref=dst,
            send_sem=self.send.at[self.count],
            recv_sem=self.recv.at[self.slot(key)],
            device_id=device,
            device_id_type=MESH,
        )
        self.count += 1
        self.started.append(copy)
        return copy

    def put(self, key, src, dst, device):
        self.prepare(key, src, dst, device).start()

    def get(self, key, dst, device):
        pltpu.make_async_remote_copy(
            src_ref=dst,
            dst_ref=dst,
            send_sem=self.send.at[0],
            recv_sem=self.recv.at[self.slot(key)],
            device_id=device,
            device_id_type=MESH,
        ).wait_recv()

    def drain(self):
        for copy in self.started:
            copy.wait_send()


def kernel(
    ts, freq, feats, w1, w2, b1, b2, g1, s1, g2, s2, tw, ew, zw, zb,
    outv,
    src, hid, xcat, acc, ctl, wt, group, stats, sums2, vin, shift, bias2, res, twv, ewv, zwv, fr,
    lsem, send, recv,
):
    x = lax.axis_index("rows")
    b = lax.axis_index("batch")
    branch = lax.axis_index("branch")
    core = b % 2
    zh = (b // 2) % 4
    y = b // 8
    label = (y + 2 * zh) % 4

    def along_x(by):
        return {"rows": (x + by) % 4}

    def along_batch(ny, nz, nc):
        return {"batch": (ny * 4 + nz) * 2 + nc}

    right, left, across = along_x(1), along_x(3), along_x(2)
    n1q = x + 1 - 2 * (x % 2)
    n2q = 3 - x
    n1, n2 = {"rows": n1q}, {"rows": n2q}
    up, down = along_batch((y + 1) % 4, zh, core), along_batch((y + 3) % 4, zh, core)
    front, back = along_batch(y, (zh + 1) % 4, core), along_batch(y, (zh + 3) % 4, core)
    twin = along_batch(y, zh, 1 - core)
    mate = {"branch": 1 - branch}

    barrier = pltpu.get_barrier_semaphore()
    for device in (right, left, across, up, down, front, back, twin, mate):
        pl.semaphore_signal(barrier, inc=1, device_id=device, device_id_type=MESH)

    local = {}

    def load(name, a, to):
        copy = pltpu.make_async_copy(a, to, lsem.at[len(local)])
        copy.start()
        local[name] = copy

    weights = (w1, w2)
    for t in range(5):
        load(f"feats{t}", feats.at[:, pl.ds(128 * t, 128)], src.at[t, pl.ds(W, POS), :])
    own_rows = pl.ds(pl.multiple_of(QC * x, 32), QC)
    load("fr", freq, fr)
    for i, ref in enumerate((b1, b2, g1, s1, g2, s2)):
        load(f"vec{i}", ref, vin.at[i])
    load("vec6", zb, vin.at[6, 0])

    pl.semaphore_wait(barrier, 9)
    net = Links(send, recv)
    put, get = net.put, net.get

    quarter = {"own": x, "N1": n1q, "N2": n2q, "F": (x + 2) % 4}
    side = {"N1": n1, "N2": n2}

    def piece(v, rel, u, d):
        row = pl.multiple_of(QC * quarter[rel] + 80 * core + 16 * u, 16)
        return wt.at[v, pl.ds(3 * d, 3), pl.ds(row, 16), :]

    def block(v, rel, c, d):
        row = pl.multiple_of(QC * quarter[rel] + 80 * c, 16)
        return wt.at[v, pl.ds(3 * d, 3), pl.ds(row, 80), :]

    def send_own(v, rel, kind, d):
        u = label if kind == "P" else 4
        a = weights[v].at[pl.ds(3 * d, 3), pl.ds(pl.multiple_of(80 * core + 16 * u, 16), 16), :]
        put((v, rel, kind, d), a, piece(v, "own", u, d), side[rel])

    def z_put(v, rel, d):
        ref = piece(v, rel, label, d)
        ahead = jnp.where((branch == 1) & (v == 1), 3, 1 if (v, rel, d) in AHEAD else 3)
        return net.prepare((v, rel, "Z", d), ref, ref, along_batch(y, (zh + ahead) % 4, core))

    late, passed = ([], []), [False, True]

    def on_piece(v, rel, d):
        ref = piece(v, rel, label, d)
        came = rel if rel != "F" else ("N1" if d < 2 else "N2")
        get((v, rel, "P", d), ref, side["N2" if came == "N1" else "N1"] if rel == "F" else side[rel])
        if rel == "N1" and d < 2:
            put((v, "F", "P", d), ref, ref, n2)
        if rel == "N2" and d == 2:
            put((v, "F", "P", d), ref, ref, n1)
        put((v, rel, "Yd", d), ref, ref, up)
        put((v, rel, "Yu", d), ref, ref, down)
        copy = z_put(v, rel, d)
        if passed[v]:
            copy.start()
        else:
            pl.when(branch == 0)(copy.start)
            late[v].append(copy)

    def z_late(v):
        passed[v] = True

        @pl.when(branch == 1)
        def _():
            for copy in late[v]:
                copy.start()

    def on_c(v, rel, d):
        ref = piece(v, rel, 4, d)
        get((v, rel, "C", d), ref, side[rel])
        if rel == "N1" and d == 0:
            put((v, "F", "C", d), ref, ref, n2)
        if rel == "N2" and d > 0:
            put((v, "F", "C", d), ref, ref, n1)

    def on_block(v, rel, d):
        if rel == "F":
            get((v, "F", "C", d), piece(v, "F", 4, d), n2 if d == 0 else n1)
        get((v, rel, "Yu", d), piece(v, rel, (label + 1) % 4, d), up)
        get((v, rel, "Yd", d), piece(v, rel, (label + 3) % 4, d), down)
        get((v, rel, "Z", d), piece(v, rel, (label + 2) % 4, d), back if (v, rel, d) in AHEAD else front)
        ref = block(v, rel, core, d)
        put((v, rel, "S", d), ref, ref, twin)

    def twin_block(v, rel, d):
        get((v, rel, "S", d), block(v, rel, 1 - core, d), twin)

    count = {"N1": 2, "N2": 1, "F": 2}

    def tile(rel, at):
        if rel == "N1":
            return jnp.where(at < 2, 0, 3)
        if rel == "N2":
            return jnp.where(at == 0, 4, jnp.where(at == 3, 0, 2))
        return (at + 2) % 4

    def tiles(rel, at):
        return pl.ds(tile(rel, at), count[rel])

    def group_matrix():
        for k in range(10):
            i = iota((64, C), 0) + 64 * k
            j = iota((64, C), 1)
            group[pl.ds(64 * k, 64), :] = jnp.where(group_of(i) == group_of(j), 1.0, 0.0).astype(BF16)

    def in_rows(total, square):
        row = iota((8, total.shape[1]), 0)
        return jnp.where(
            row == 0,
            jnp.sum(total, axis=0, keepdims=True),
            jnp.where(row == 1, jnp.sum(square, axis=0, keepdims=True), 0.0),
        )

    def moments(total):
        both = exact_dot(total, group[...]) * (1.0 / COUNT)
        mean = both[0:1]
        var = both[1:2] - mean * mean
        return mean, lax.rsqrt(var + 1e-05)

    def halo(buf, t, key):
        put((key, "top"), buf.at[t(x), pl.ds(POS, W), :], buf.at[t(x), pl.ds(0, W), :], right)
        put((key, "end"), buf.at[t(x), pl.ds(W, W), :], buf.at[t(x), pl.ds(POS + W, W), :], left)

    def wait_halo(buf, t, key):
        get((key, "top"), buf.at[t((x + 3) % 4), pl.ds(0, W), :], left)
        get((key, "end"), buf.at[t((x + 1) % 4), pl.ds(POS + W, W), :], right)

    def all_tiles(at):
        return pl.ds(0, 5)

    def activate(buf, mean, scale, shift):
        def step(i, _):
            rows = pl.ds(pl.multiple_of(W * i, W), W)
            outside = ((i == 0) & (x == 0)) | ((i == 9) & (x == 3))
            keep = jnp.where(outside, 0.0, 1.0)
            col = iota((W, 128), 0)
            for t in range(5):
                lanes = slice(128 * t, 128 * t + 128)
                v = buf[t, rows, :].astype(F32)
                a = silu((v - mean[:, lanes]) * scale[:, lanes] + shift[:, lanes]) * keep
                first = jnp.where(col == 0, 0.0, pltpu.roll(a, 1, 0))
                last = jnp.where(col == W - 1, 0.0, pltpu.roll(a, W - 1, 0))
                for k, part in enumerate((first, a, last)):
                    xcat[rows, pl.ds(C * k + 128 * t, 128)] = part.astype(BF16)
            return 0

        lax.fori_loop(0, 10, step, 0)

    def conv(v, t, n, d):
        rows = pl.ds(pl.multiple_of(128 * t, 128), 128 * n)
        rhs = jnp.concatenate([wt[v, 3 * d + k, rows, :] for k in range(3)], axis=1)
        for i in range(2):
            half = pl.ds(POS // 2 * i, POS // 2)
            lhs = xcat[pl.ds(W * d + POS // 2 * i, POS // 2), :]
            r = lax.dot_general(lhs, rhs, (((1,), (1,)), ((), ())), preferred_element_type=F32)
            for k in range(n):
                part = r[:, 128 * k : 128 * k + 128]
                acc[t + k, half, :] = part if d == 0 else acc[t + k, half, :] + part

    def add_up(values):
        total, square = 0.0, 0.0
        for k in range(values.shape[0] // 8):
            part = values[8 * k : 8 * k + 8]
            total, square = total + part, square + part * part
        return total, square

    def do_edges():
        halo(src, all_tiles, "features")

    def do_stats():
        load("tw", tw, twv)
        load("ew", ew, ewv)
        load("own0", w1, wt.at[0, :, own_rows, :])
        for t in range(5):
            local[f"feats{t}"].wait()

        def step(i, carry):
            rows = pl.ds(pl.multiple_of(W + W * i, W), W)
            new = []
            for t in range(5):
                total, square = add_up(src[t, rows, :].astype(F32))
                new += [carry[2 * t] + total, carry[2 * t + 1] + square]
            return tuple(new)

        carry = lax.fori_loop(0, HR, step, (jnp.zeros((8, 128), F32),) * 10)
        stats[x] = in_rows(jnp.concatenate(carry[0::2], axis=1), jnp.concatenate(carry[1::2], axis=1))
        group_matrix()
        for by, device in ((1, right), (2, across), (3, left)):
            put(("stats", by), stats.at[x], stats.at[x], device)
        load("own1", w2, wt.at[1, :, own_rows, :])
        load("zw", zw, zwv)

    def do_time():
        for i in range(7):
            local[f"vec{i}"].wait()
        local["fr"].wait()
        local["tw"].wait()
        local["ew"].wait()
        angle = jnp.broadcast_to(fr[...] * ts[0].astype(F32), (8, 320))
        n = jnp.floor(angle * (2.0 / math.pi) + 0.5)
        r = ((angle - n * 1.5703125) - n * 4.837512969970703e-4) - n * 7.549790126404332e-8
        turn = n + jnp.where(iota((8, 320), 1) < 160, 1.0, 0.0)
        turn = turn - 4.0 * jnp.floor(turn * 0.25)
        r2 = r * r
        sin_r = r + r * r2 * (-1.0 / 6 + r2 * (1.0 / 120 + r2 * (-1.0 / 5040 + r2 * (1.0 / 362880))))
        cos_r = 1.0 + r2 * (-0.5 + r2 * (1.0 / 24 + r2 * (-1.0 / 720 + r2 * (1.0 / 40320 - r2 * (1.0 / 3628800)))))
        waves = jnp.where(
            turn < 0.5, sin_r, jnp.where(turn < 1.5, cos_r, jnp.where(turn < 2.5, -sin_r, -cos_r))
        )
        inner = silu(exact_dot(waves, twv[...]))
        extra = vin[0] + exact_dot(inner, ewv[...])
        for t in range(5):
            shift[t] = extra[:, 128 * t : 128 * t + 128]
            bias2[t] = jnp.broadcast_to(vin[1][:, 128 * t : 128 * t + 128], (8, 128))

    def do_first():
        wait_halo(src, all_tiles, "features")
        for by, device in ((1, left), (2, across), (3, right)):
            get(("stats", by), stats.at[(x - by + 4) % 4], device)
        mean, scale = moments(stats[0] + stats[1] + stats[2] + stats[3])
        activate(src, mean, scale * vin[2], vin[3])

    def do_hidden(rel):
        for k in range(count[rel]):
            t = tile(rel, x) + k

            def step(i, carry):
                rows = pl.ds(pl.multiple_of(W * i, W), W)
                h = (acc[t, rows, :] + shift[t][0:1]).astype(BF16)
                hid[t, pl.ds(pl.multiple_of(W + W * i, W), W), :] = h
                total, square = add_up(h.astype(F32))
                return carry[0] + total, carry[1] + square

            zero = jnp.zeros((8, 128), F32)
            total, square = lax.fori_loop(0, HR, step, (zero, zero))
            sums2[x, t] = in_rows(total, square)
        halo(hid, lambda at: tiles(rel, at), ("hidden", rel))
        ref = sums2.at[x, tiles(rel, x)]
        for by, device in ((1, right), (2, across), (3, left)):
            put(("sums", rel, by), ref, ref, device)

    def do_second():
        for rel in ("N1", "N2", "F"):
            wait_halo(hid, lambda at: tiles(rel, at), ("hidden", rel))
            for by, device in ((1, left), (2, across), (3, right)):
                at = (x - by + 4) % 4
                get(("sums", rel, by), sums2.at[at, tiles(rel, at)], device)
        total = [sums2[0, t] + sums2[1, t] + sums2[2, t] + sums2[3, t] for t in range(5)]
        mean, scale = moments(jnp.concatenate(total, axis=1))
        activate(hid, mean, scale * vin[4], vin[5])

    slots = {"N1": 0, "N2": 2, "F": 3}

    def ctl_copy(rel, k):
        t = tile(rel, x) + k
        slot = CTL + slots[rel] + k
        return pltpu.make_async_remote_copy(
            src_ref=ctl.at[t],
            dst_ref=ctl.at[t],
            send_sem=send.at[slot],
            recv_sem=recv.at[slot],
            device_id=mate,
            device_id_type=MESH,
        )

    def pre(t, rows):
        own = src[t, pl.ds(W + rows.start, rows.size), :].astype(F32)
        return own + acc[t, rows, :] + bias2[t][0:1]

    def give(rel):
        @pl.when(branch == 0)
        def _():
            for k in range(count[rel]):
                t = tile(rel, x) + k
                ctl[t] = pre(t, pl.ds(0, POS)).astype(BF16)
                ctl_copy(rel, k).start()

    def do_conv(v, rel, d):
        if rel == "N1" and d == 0:
            local[f"own{v}"].wait()
        twin_block(v, rel, d)
        conv(v, tile(rel, x), count[rel], d)
        if v == 1 and d == 2:
            give(rel)

    steps = {
        "own": send_own,
        "piece": on_piece,
        "c": on_c,
        "block": on_block,
        "conv": do_conv,
        "zlate0": lambda: z_late(0),
        "edges": do_edges,
        "stats": do_stats,
        "time": do_time,
        "first": do_first,
        "hidden": do_hidden,
        "second": do_second,
    }
    for step in ORDER:
        steps[step[0]](*step[1:])
    local["zw"].wait()

    @pl.when(branch == 1)
    def _():
        for rel in ("N1", "N2", "F"):
            n = count[rel]
            t = tile(rel, x)
            for k in range(n):
                ctl_copy(rel, k).wait_recv()

            def step(i, _):
                rows = pl.ds(pl.multiple_of(128 * i, 128), 128)
                lhs = jnp.concatenate([ctl[t + k, rows, :] for k in range(n)], axis=1)
                rhs = zwv[pl.ds(pl.multiple_of(128 * t, 128), 128 * n), :]
                r = jnp.dot(lhs, rhs, preferred_element_type=F32)
                if rel == "N1":
                    res[rows, :] = r + vin[6]
                elif rel == "N2":
                    res[rows, :] = res[rows, :] + r
                else:
                    r = (res[rows, :] + r).astype(BF16).astype(F32)
                    for k in range(5):
                        lanes = slice(128 * k, 128 * k + 128)
                        outv[rows, pl.ds(128 * k, 128)] = (pre(k, rows) + r[:, lanes]).astype(BF16)
                return 0

            lax.fori_loop(0, 4, step, 0)

    @pl.when(branch == 0)
    def _():
        for t in range(5):
            outv[:, pl.ds(128 * t, 128)] = ctl[t]
        for rel in ("N1", "N2", "F"):
            for k in range(count[rel]):
                ctl_copy(rel, k).wait_send()

    net.drain()


def body(
    timestep,
    features,
    conv1_weight,
    conv1_bias,
    conv2_weight,
    conv2_bias,
    norm1_gain,
    norm1_shift,
    norm2_gain,
    norm2_shift,
    time_weight,
    emb_weight,
    zero_weight,
    zero_bias,
):
    half = 160
    line = np.exp(-math.log(10000.0) * np.arange(half, dtype=np.float32) / np.float32(half))
    freq = jnp.asarray(np.concatenate([line, line])[None].astype(np.float32))
    hbm = pl.BlockSpec(memory_space=pltpu.HBM)
    vmem = pltpu.VMEM
    result = pl.pallas_call(
        kernel,
        out_shape=pltpu.VMEM((POS, C), BF16),
        in_specs=[pl.BlockSpec(memory_space=pltpu.SMEM)] + [hbm] * 14,
        out_specs=pl.BlockSpec(memory_space=pltpu.VMEM),
        scratch_shapes=[
            vmem((5, POS + 2 * W, 128), BF16),
            vmem((5, POS + 2 * W, 128), BF16),
            vmem((POS + 2 * W, 3 * C), BF16),
            vmem((5, POS, 128), F32),
            vmem((5, POS, 128), BF16),
            vmem((2, 9, C, C), BF16),
            vmem((C, C), BF16),
            vmem((4, 8, C), F32),
            vmem((4, 5, 8, 128), F32),
            vmem((7, 1, C), F32),
            vmem((5, 8, 128), F32),
            vmem((5, 8, 128), F32),
            vmem((POS, C), F32),
            vmem((320, 1280), BF16),
            vmem((1280, C), BF16),
            vmem((C, C), BF16),
            vmem((1, 320), F32),
            pltpu.SemaphoreType.DMA((20,)),
            pltpu.SemaphoreType.DMA((CTL + 5,)),
            pltpu.SemaphoreType.DMA((CTL + 5,)),
        ],
        compiler_params=pltpu.CompilerParams(
            collective_id=0, has_side_effects=True, vmem_limit_bytes=60 * 1024 * 1024
        ),
        name="block",
    )(
        timestep,
        freq,
        features.reshape(POS, C),
        jnp.swapaxes(conv1_weight, 3, 4).reshape(9, QC, C),
        jnp.swapaxes(conv2_weight, 3, 4).reshape(9, QC, C),
        conv1_bias,
        conv2_bias,
        norm1_gain,
        norm1_shift,
        norm2_gain,
        norm2_shift,
        time_weight[0],
        emb_weight[0],
        zero_weight,
        zero_bias,
    )
    return result.reshape(1, 1, HR, W, C)


def solution(mesh):
    placed = (
        P("batch"),
        P("batch", "branch", "rows", None, None),
        P("branch", None, None, None, "rows"),
        P("branch", None),
        P("branch", None, None, None, "rows"),
        P("branch", None),
        P("branch", None),
        P("branch", None),
        P("branch", None),
        P("branch", None),
        P("branch", None, None),
        P("branch", None, None),
        P(),
        P(),
    )
    return jax.shard_map(
        body,
        mesh=mesh,
        in_specs=placed,
        out_specs=P("batch", "branch", "rows", None, None),
        check_vma=False,
    )
```

profile of v0, /device:TPU:32, one launch (start us, length us, event | category | flops | bytes accessed | tf_op | source)
XLA Modules:
  0.0 62.3 jit_solution(16597824713765614838)
XLA Ops:
  0.7 60.8 %block.1 = bf16[512,640]{1,0:T(8,128)(2,1)S(1)} custom-call(s32[1]{0:T(128)S(6)} %copy.18.ts, f32[1,320]{1,0:T(1,128)} %constant.2.clone.freq, bf16[512,640]{1,0:T(8,128)(2,1)} %bitcast.15, bf16[9,160,640]{2,1,0:T(8,128)(2,1)} %bitcast.11, bf16[9,160,640]{2,1,0:T(8,128)(2,1)} %bitcast.12, f32[1,640]{1,0:T(1,128)} %b1.1, f32[1,640]{1,0:T(1,128)} %b2.1, ...), custom_call_target="tpu_custom_call" | custom-call | tf_op jit(solution)/shard_map/block/pallas_call | solution.py:600
  61.5 0.8 %copy.17 = bf16[1,1,8,64,640]{4,3,2,1,0:T(8,128)(2,1)} copy(bf16[1,1,8,64,640]{4,3,2,1,0:T(8,128)(2,1)S(1)} %bitcast.10) | data formatting | bytes 1310720
where the time goes:
time: 62.4 us; the launch traced here: 62.3 us
  Pallas kernels  60.8 us (97%)
  local copies, waits for them, and re-layouts  0.84 us (1%)
  between operations  0.66 us (1%)
    pallas_call x1, Pallas kernels, body(): pl.pallas_call(kernel, out_shape=pltpu.VMEM((POS, C), BF16), in_specs=[pl...  60.8 us

commit v1 on v0

--- a/solution.py
+++ b/solution.py
@@ -23,118 +23,141 @@
 BF16 = jnp.bfloat16
 
 
+OWN = "own"
+PIECE = "piece"
+REST = "c"
+BLOCK = "block"
+CONV = "conv"
+FORWARD = "fwd"
+LATE = "zlate0"
+EDGES = "edges"
+STATS = "stats"
+TIME = "time"
+FIRST = "first"
+HIDDEN = "hidden"
+SECOND = "second"
+N1 = "N1"
+N2 = "N2"
+FAR = "F"
+MAIN = "P"
+LAST = "C"
 ORDER = (
-    ("own", 0, "N1", "P", 0),
-    ("own", 0, "N2", "P", 0),
-    ("own", 0, "N1", "P", 1),
-    ("own", 0, "N2", "P", 1),
-    ("own", 0, "N1", "P", 2),
-    ("own", 0, "N2", "P", 2),
-    ("stats",),
-    ("time",),
-    ("piece", 0, "N1", 0),
-    ("piece", 0, "N2", 0),
-    ("piece", 0, "N1", 1),
-    ("piece", 0, "N2", 1),
-    ("edges",),
-    ("piece", 0, "N1", 2),
-    ("piece", 0, "N2", 2),
-    ("own", 0, "N1", "C", 0),
-    ("own", 0, "N2", "C", 0),
-    ("own", 0, "N1", "C", 1),
-    ("own", 0, "N2", "C", 1),
-    ("own", 0, "N1", "C", 2),
-    ("own", 0, "N2", "C", 2),
-    ("own", 1, "N1", "P", 0),
-    ("own", 1, "N2", "P", 0),
-    ("piece", 0, "F", 0),
-    ("piece", 0, "F", 1),
-    ("piece", 0, "F", 2),
-    ("first",),
-    ("c", 0, "N1", 0),
-    ("c", 0, "N2", 0),
-    ("zlate0",),
-    ("block", 0, "N1", 0),
-    ("block", 0, "N2", 0),
-    ("c", 0, "N1", 1),
-    ("block", 0, "N1", 1),
-    ("c", 0, "N2", 1),
-    ("block", 0, "N2", 1),
-    ("conv", 0, "N1", 0),
-    ("c", 0, "N1", 2),
-    ("c", 0, "N2", 2),
-    ("block", 0, "N1", 2),
-    ("block", 0, "N2", 2),
-    ("own", 1, "N1", "P", 2),
-    ("own", 1, "N2", "P", 1),
-    ("conv", 0, "N1", 1),
-    ("piece", 1, "N1", 0),
-    ("conv", 0, "N2", 0),
-    ("piece", 1, "N2", 0),
-    ("conv", 0, "N1", 2),
-    ("block", 0, "F", 0),
-    ("block", 0, "F", 1),
-    ("hidden", "N1"),
-    ("conv", 0, "N2", 1),
-    ("block", 0, "F", 2),
-    ("own", 1, "N1", "P", 1),
-    ("own", 1, "N2", "P", 2),
-    ("own", 1, "N1", "C", 0),
-    ("own", 1, "N2", "C", 1),
-    ("piece", 1, "N2", 1),
-    ("conv", 0, "N2", 2),
-    ("hidden", "N2"),
-    ("piece", 1, "N1", 2),
-    ("conv", 0, "F", 0),
-    ("piece", 1, "F", 0),
-    ("conv", 0, "F", 1),
-    ("conv", 0, "F", 2),
-    ("hidden", "F"),
-    ("piece", 1, "N1", 1),
-    ("own", 1, "N1", "C", 1),
-    ("own", 1, "N2", "C", 0),
-    ("own", 1, "N1", "C", 2),
-    ("own", 1, "N2", "C", 2),
-    ("piece", 1, "N2", 2),
-    ("c", 1, "N1", 0),
-    ("block", 1, "N1", 0),
-    ("c", 1, "N2", 1),
-    ("block", 1, "N2", 1),
-    ("second",),
-    ("c", 1, "N1", 1),
-    ("piece", 1, "F", 1),
-    ("block", 1, "N1", 1),
-    ("conv", 1, "N1", 0),
-    ("c", 1, "N1", 2),
-    ("block", 1, "N1", 2),
-    ("c", 1, "N2", 0),
-    ("block", 1, "N2", 0),
-    ("conv", 1, "N1", 1),
-    ("c", 1, "N2", 2),
-    ("piece", 1, "F", 2),
-    ("block", 1, "N2", 2),
-    ("conv", 1, "N1", 2),
-    ("conv", 1, "N2", 0),
-    ("block", 1, "F", 0),
-    ("conv", 1, "N2", 1),
-    ("conv", 1, "N2", 2),
-    ("block", 1, "F", 1),
-    ("conv", 1, "F", 0),
-    ("conv", 1, "F", 1),
-    ("block", 1, "F", 2),
-    ("conv", 1, "F", 2),
+    (OWN, 0, N1, MAIN, 1),
+    (OWN, 0, N2, MAIN, 2),
+    (OWN, 0, N1, MAIN, 2),
+    (OWN, 0, N2, MAIN, 0),
+    (OWN, 0, N2, LAST, 0),
+    (OWN, 0, N1, MAIN, 0),
+    (OWN, 0, N1, LAST, 2),
+    (OWN, 0, N2, MAIN, 1),
+    (STATS,),
+    (OWN, 0, N1, LAST, 0),
+    (OWN, 0, N2, LAST, 2),
+    (TIME,),
+    (OWN, 0, N2, LAST, 1),
+    (PIECE, 0, N2, 2),
+    (PIECE, 0, N1, 2),
+    (PIECE, 0, N1, 0),
+    (OWN, 0, N1, LAST, 1),
+    (OWN, 1, N1, MAIN, 0),
+    (PIECE, 0, N2, 1),
+    (REST, 0, N1, 2),
+    (PIECE, 0, N1, 1),
+    (EDGES,),
+    (OWN, 1, N2, MAIN, 2),
+    (PIECE, 0, N2, 0),
+    (OWN, 1, N1, MAIN, 1),
+    (LATE,),
+    (BLOCK, 0, N1, 2),
+    (PIECE, 0, FAR, 0),
+    (REST, 0, N1, 0),
+    (OWN, 1, N1, MAIN, 2),
+    (REST, 0, N2, 1),
+    (PIECE, 0, FAR, 1),
+    (PIECE, 0, FAR, 2),
+    (OWN, 1, N2, MAIN, 0),
+    (BLOCK, 0, N1, 0),
+    (BLOCK, 0, N2, 1),
+    (REST, 0, N1, 1),
+    (OWN, 1, N2, MAIN, 1),
+    (REST, 0, N2, 2),
+    (REST, 0, N2, 0),
+    (BLOCK, 0, N1, 1),
+    (OWN, 1, N2, LAST, 2),
+    (PIECE, 1, N1, 0),
+    (FIRST,),
+    (BLOCK, 0, N2, 0),
+    (OWN, 1, N1, LAST, 2),
+    (CONV, 0, N1, 0),
+    (OWN, 1, N2, LAST, 1),
+    (PIECE, 1, N2, 2),
+    (OWN, 1, N2, LAST, 0),
+    (BLOCK, 0, N2, 2),
+    (CONV, 0, N1, 1),
+    (OWN, 1, N1, LAST, 0),
+    (OWN, 1, N1, LAST, 1),
+    (CONV, 0, N1, 2),
+    (BLOCK, 0, FAR, 0),
+    (CONV, 0, N2, 0),
+    (PIECE, 1, N1, 2),
+    (PIECE, 1, N1, 1),
+    (HIDDEN, N1),
+    (FORWARD, N2, 2),
+    (BLOCK, 0, FAR, 1),
+    (FORWARD, N1, 0),
+    (CONV, 0, N2, 1),
+    (BLOCK, 0, FAR, 2),
+    (CONV, 0, N2, 2),
+    (CONV, 0, FAR, 0),
+    (PIECE, 1, N2, 0),
+    (HIDDEN, N2),
+    (CONV, 0, FAR, 1),
+    (CONV, 0, FAR, 2),
+    (HIDDEN, FAR),
+    (PIECE, 1, N2, 1),
+    (REST, 1, N2, 1),
+    (FORWARD, N1, 1),
+    (REST, 1, N1, 0),
+    (BLOCK, 1, N1, 0),
+    (PIECE, 1, FAR, 0),
+    (REST, 1, N2, 2),
+    (REST, 1, N1, 2),
+    (REST, 1, N2, 0),
+    (REST, 1, N1, 1),
+    (BLOCK, 1, N1, 1),
+    (PIECE, 1, FAR, 2),
+    (BLOCK, 1, N1, 2),
+    (BLOCK, 1, N2, 0),
+    (SECOND,),
+    (PIECE, 1, FAR, 1),
+    (BLOCK, 1, N2, 1),
+    (CONV, 1, N1, 0),
+    (CONV, 1, N1, 1),
+    (CONV, 1, N1, 2),
+    (BLOCK, 1, FAR, 0),
+    (BLOCK, 1, FAR, 2),
+    (CONV, 1, N2, 0),
+    (BLOCK, 1, N2, 2),
+    (CONV, 1, N2, 1),
+    (BLOCK, 1, FAR, 1),
+    (CONV, 1, FAR, 0),
+    (CONV, 1, N2, 2),
+    (CONV, 1, FAR, 1),
+    (CONV, 1, FAR, 2),
 )
 AHEAD = {
-    (0, "N1", 2),
-    (0, "N2", 2),
-    (0, "F", 1),
-    (0, "F", 2),
-    (1, "N1", 0),
-    (1, "N1", 1),
-    (1, "N1", 2),
-    (1, "N2", 0),
-    (1, "N2", 1),
-    (1, "N2", 2),
+    (0, FAR, 2),
+    (0, N1, 2),
+    (0, N2, 1),
+    (1, FAR, 0),
+    (1, FAR, 1),
+    (1, FAR, 2),
+    (1, N1, 0),
+    (1, N1, 1),
+    (1, N1, 2),
+    (1, N2, 0),
+    (1, N2, 1),
+    (1, N2, 2),
 }
 
 
@@ -278,14 +301,19 @@
 
     late, passed = ([], []), [False, True]
 
+    def forward(v, rel, d):
+        ref = piece(v, rel, label, d)
+        if rel == "N1" and d < 2:
+            put((v, "F", "P", d), ref, ref, n2)
+        if rel == "N2" and d == 2:
+            put((v, "F", "P", d), ref, ref, n1)
+
     def on_piece(v, rel, d):
         ref = piece(v, rel, label, d)
         came = rel if rel != "F" else ("N1" if d < 2 else "N2")
         get((v, rel, "P", d), ref, side["N2" if came == "N1" else "N1"] if rel == "F" else side[rel])
-        if rel == "N1" and d < 2:
-            put((v, "F", "P", d), ref, ref, n2)
-        if rel == "N2" and d == 2:
-            put((v, "F", "P", d), ref, ref, n1)
+        if v == 0:
+            forward(v, rel, d)
         put((v, rel, "Yd", d), ref, ref, up)
         put((v, rel, "Yu", d), ref, ref, down)
         copy = z_put(v, rel, d)
@@ -489,12 +517,13 @@
 
     slots = {"N1": 0, "N2": 2, "F": 3}
 
-    def ctl_copy(rel, k):
+    def ctl_copy(rel, k, half):
         t = tile(rel, x) + k
-        slot = CTL + slots[rel] + k
+        slot = CTL + 2 * (slots[rel] + k) + half
+        ref = ctl.at[t, pl.ds(POS // 2 * half, POS // 2), :]
         return pltpu.make_async_remote_copy(
-            src_ref=ctl.at[t],
-            dst_ref=ctl.at[t],
+            src_ref=ref,
+            dst_ref=ref,
             send_sem=send.at[slot],
             recv_sem=recv.at[slot],
             device_id=mate,
@@ -511,7 +540,13 @@
             for k in range(count[rel]):
                 t = tile(rel, x) + k
                 ctl[t] = pre(t, pl.ds(0, POS)).astype(BF16)
-                ctl_copy(rel, k).start()
+                if rel != "F":
+                    for half in range(2):
+                        ctl_copy(rel, k, half).start()
+            if rel == "F":
+                for half in range(2):
+                    for k in range(2):
+                        ctl_copy(rel, k, half).start()
 
     def do_conv(v, rel, d):
         if rel == "N1" and d == 0:
@@ -525,6 +560,7 @@
         "own": send_own,
         "piece": on_piece,
         "c": on_c,
+        "fwd": lambda rel, d: forward(1, rel, d),
         "block": on_block,
         "conv": do_conv,
         "zlate0": lambda: z_late(0),
@@ -544,8 +580,10 @@
         for rel in ("N1", "N2", "F"):
             n = count[rel]
             t = tile(rel, x)
-            for k in range(n):
-                ctl_copy(rel, k).wait_recv()
+
+            def arrive(half):
+                for k in range(n):
+                    ctl_copy(rel, k, half).wait_recv()
 
             def step(i, _):
                 rows = pl.ds(pl.multiple_of(128 * i, 128), 128)
@@ -563,7 +601,9 @@
                         outv[rows, pl.ds(128 * k, 128)] = (pre(k, rows) + r[:, lanes]).astype(BF16)
                 return 0
 
-            lax.fori_loop(0, 4, step, 0)
+            for half in range(2):
+                arrive(half)
+                lax.fori_loop(2 * half, 2 * half + 2, step, 0)
 
     @pl.when(branch == 0)
     def _():
@@ -571,7 +611,8 @@
             outv[:, pl.ds(128 * t, 128)] = ctl[t]
         for rel in ("N1", "N2", "F"):
             for k in range(count[rel]):
-                ctl_copy(rel, k).wait_send()
+                for half in range(2):
+                    ctl_copy(rel, k, half).wait_send()
 
     net.drain()
 
@@ -621,8 +662,8 @@
             vmem((C, C), BF16),
             vmem((1, 320), F32),
             pltpu.SemaphoreType.DMA((20,)),
-            pltpu.SemaphoreType.DMA((CTL + 5,)),
-            pltpu.SemaphoreType.DMA((CTL + 5,)),
+            pltpu.SemaphoreType.DMA((CTL + 10,)),
+            pltpu.SemaphoreType.DMA((CTL + 10,)),
         ],
         compiler_params=pltpu.CompilerParams(
             collective_id=0, has_side_effects=True, vmem_limit_bytes=60 * 1024 * 1024

time: 62.4 us -> 60 us (0.962)
  Pallas kernels: 60.8 us -> 58.4 us
    pallas_call x1, Pallas kernels: 60.8 us -> 58.4 us  [body(): pl.pallas_call(kernel, out_shape=pltpu.VMEM((POS, C), BF16), in_specs=[pl...]
where the time goes in v1:
time: 60 us; the launch traced here: 59.9 us
  Pallas kernels  58.4 us (97%)
  local copies, waits for them, and re-layouts  0.84 us (1%)
  between operations  0.66 us (1%)
    pallas_call x1, Pallas kernels, body(): pl.pallas_call(kernel, out_shape=pltpu.VMEM((POS, C), BF16), in_specs=[pl...  58.4 us

profile of v1, /device:TPU:32, one launch (start us, length us, event | category | flops | bytes accessed | tf_op | source)
XLA Modules:
  0.0 59.9 jit_solution(3758129140131932029)
XLA Ops:
  0.7 58.4 %block.1 = bf16[512,640]{1,0:T(8,128)(2,1)S(1)} custom-call(s32[1]{0:T(128)S(6)} %copy.18.ts, f32[1,320]{1,0:T(1,128)} %constant.2.clone.freq, bf16[512,640]{1,0:T(8,128)(2,1)} %bitcast.15, bf16[9,160,640]{2,1,0:T(8,128)(2,1)} %bitcast.11, bf16[9,160,640]{2,1,0:T(8,128)(2,1)} %bitcast.12, f32[1,640]{1,0:T(1,128)} %b1.1, f32[1,640]{1,0:T(1,128)} %b2.1, ...), custom_call_target="tpu_custom_call" | custom-call | tf_op jit(solution)/shard_map/block/pallas_call | solution.py:641
  59.0 0.8 %copy.17 = bf16[1,1,8,64,640]{4,3,2,1,0:T(8,128)(2,1)} copy(bf16[1,1,8,64,640]{4,3,2,1,0:T(8,128)(2,1)S(1)} %bitcast.10) | data formatting | bytes 1310720

commit v2 on v1

--- a/solution.py
+++ b/solution.py
@@ -519,8 +519,8 @@
 
     def ctl_copy(rel, k, half):
         t = tile(rel, x) + k
-        slot = CTL + 2 * (slots[rel] + k) + half
-        ref = ctl.at[t, pl.ds(POS // 2 * half, POS // 2), :]
+        slot = CTL + 4 * (slots[rel] + k) + half
+        ref = ctl.at[t, pl.ds(POS // 4 * half, POS // 4), :]
         return pltpu.make_async_remote_copy(
             src_ref=ref,
             dst_ref=ref,
@@ -541,10 +541,10 @@
                 t = tile(rel, x) + k
                 ctl[t] = pre(t, pl.ds(0, POS)).astype(BF16)
                 if rel != "F":
-                    for half in range(2):
+                    for half in range(4):
                         ctl_copy(rel, k, half).start()
             if rel == "F":
-                for half in range(2):
+                for half in range(4):
                     for k in range(2):
                         ctl_copy(rel, k, half).start()
 
@@ -601,9 +601,9 @@
                         outv[rows, pl.ds(128 * k, 128)] = (pre(k, rows) + r[:, lanes]).astype(BF16)
                 return 0
 
-            for half in range(2):
+            for half in range(4):
                 arrive(half)
-                lax.fori_loop(2 * half, 2 * half + 2, step, 0)
+                lax.fori_loop(half, half + 1, step, 0)
 
     @pl.when(branch == 0)
     def _():
@@ -611,7 +611,7 @@
             outv[:, pl.ds(128 * t, 128)] = ctl[t]
         for rel in ("N1", "N2", "F"):
             for k in range(count[rel]):
-                for half in range(2):
+                for half in range(4):
                     ctl_copy(rel, k, half).wait_send()
 
     net.drain()
@@ -662,8 +662,8 @@
             vmem((C, C), BF16),
             vmem((1, 320), F32),
             pltpu.SemaphoreType.DMA((20,)),
-            pltpu.SemaphoreType.DMA((CTL + 10,)),
-            pltpu.SemaphoreType.DMA((CTL + 10,)),
+            pltpu.SemaphoreType.DMA((CTL + 20,)),
+            pltpu.SemaphoreType.DMA((CTL + 20,)),
         ],
         compiler_params=pltpu.CompilerParams(
             collective_id=0, has_side_effects=True, vmem_limit_bytes=60 * 1024 * 1024

time: 60 us -> 59.9 us (level)
  no operation moved by 1% of the time
where the time goes in v2:
time: 59.9 us; the launch traced here: 59.8 us
  Pallas kernels  58.3 us (97%)
  local copies, waits for them, and re-layouts  0.84 us (1%)
  between operations  0.66 us (1%)
    pallas_call x1, Pallas kernels, body(): pl.pallas_call(kernel, out_shape=pltpu.VMEM((POS, C), BF16), in_specs=[pl...  58.3 us

profile of v2, /device:TPU:32, one launch (start us, length us, event | category | flops | bytes accessed | tf_op | source)
XLA Modules:
  0.0 59.8 jit_solution(7508258548687965415)
XLA Ops:
  0.7 58.3 %block.1 = bf16[512,640]{1,0:T(8,128)(2,1)S(1)} custom-call(s32[1]{0:T(128)S(6)} %copy.18.ts, f32[1,320]{1,0:T(1,128)} %constant.2.clone.freq, bf16[512,640]{1,0:T(8,128)(2,1)} %bitcast.15, bf16[9,160,640]{2,1,0:T(8,128)(2,1)} %bitcast.11, bf16[9,160,640]{2,1,0:T(8,128)(2,1)} %bitcast.12, f32[1,640]{1,0:T(1,128)} %b1.1, f32[1,640]{1,0:T(1,128)} %b2.1, ...), custom_call_target="tpu_custom_call" | custom-call | tf_op jit(solution)/shard_map/block/pallas_call | solution.py:641
  59.0 0.8 %copy.17 = bf16[1,1,8,64,640]{4,3,2,1,0:T(8,128)(2,1)} copy(bf16[1,1,8,64,640]{4,3,2,1,0:T(8,128)(2,1)S(1)} %bitcast.10) | data formatting | bytes 1310720
